TPU v7x, 256 devices: a whole 4x4x8 slice. The times are simulated.
256 devices in a mesh: dp: 8 (over z), expert: 32 (over x, y, core).
Axes of the slice: x: 4, y: 4, z: 8, core: 2. Of those that a mesh axis runs over, the one named last changes fastest.
Arguments:
- tokens: bfloat16 [65536, 2048], P(('dp', 'expert')), may hold values from -6 to 6
- expert_ranks: int32 [32, 65536], P(None, ('dp', 'expert')), may hold values from 0 to 65535, as said below
- capacity: int32 [32], replicated, may hold values from 512 to 1024, as said below
- weight_in: bfloat16 [32, 2048, 8192], P('expert', None, 'dp'), may hold values from -0.125 to 0.125
- weight_out: bfloat16 [32, 8192, 2048], P('expert', 'dp'), may hold values from -0.0625 to 0.0625
- gate_weights: float32 [32, 1024], P('expert', 'dp'), may hold values from 0.05 to 1
Outputs:
- combined: bfloat16 [65536, 2048], P(('dp', 'expert'))
Inputs may be any that keep to these rules, and one draw needn't show every extreme that they name: `expert_ranks`: for each expert the ranks are a permutation of 0 to 65535. Of the 256 tokens of one device, at most 8 have rank under 1024 for one expert; for an expert of capacity 1024, some devices have exactly 8. At least one expert has capacity 1024.
All inputs are finite; a program needn't handle non-finite values.
Results may differ from a plain program's by a relative error of at most 0.0053.
Values may be sent and summed in bfloat16 or wider, within the bound.
No kernel may reach another device: no remote copies, remote signals or barrier semaphores. Data moves between devices by JAX's collectives and lax.ppermute only.
A program may use at most 64 MiB of HBM per device.

v0:
```python
import jax
import jax.numpy as jnp
from jax import lax
from jax.sharding import Mesh
from jax.sharding import PartitionSpec as P

MOST = 8
EXPERT = ("expert_0", "expert_1", "expert_2")
DP_EXPERT = ("dp", "expert_0", "expert_1", "expert_2")


def exclusive(values):
    return jnp.cumsum(values) - values


def on_device(tokens, expert_ranks, capacity, weight_in, weight_out, gate_weights):
    dp_count = lax.axis_size("dp")
    expert_count = lax.axis_size(EXPERT)
    token_count, width = tokens.shape
    slots_dp = gate_weights.shape[1]
    rows_all = expert_count * MOST
    own_dp = lax.axis_index("dp")
    own_expert = lax.axis_index(EXPERT)
    chosen = expert_ranks < capacity[:, None]
    chosen_int = chosen.astype(jnp.int32)
    counts = jnp.sum(chosen_int, axis=1)
    before = jnp.cumsum(chosen_int, axis=1) - chosen_int
    places = lax.broadcasted_iota(jnp.int32, (expert_count, MOST, token_count), 1)
    pack_table = jnp.logical_and(chosen[:, None, :], before[:, None, :] == places)
    pack_table = pack_table.astype(jnp.bfloat16).reshape(rows_all, token_count)
    packed = jnp.dot(pack_table, tokens, preferred_element_type=jnp.float32).astype(jnp.bfloat16)
    arrived_rows = lax.all_to_all(
        packed.reshape(expert_count, MOST, width), EXPERT, split_axis=0, concat_axis=0, tiled=True
    ).reshape(rows_all, width)
    device_ids = lax.broadcasted_iota(jnp.int32, (expert_count, expert_count), 0)
    expert_ids = lax.broadcasted_iota(jnp.int32, (expert_count, expert_count), 1)
    table = lax.psum(jnp.where(device_ids == own_expert, counts[None, :], 0), EXPERT)
    plane_ids = lax.broadcasted_iota(jnp.int32, (dp_count, expert_count), 0)
    plane_counts = lax.psum(
        jnp.where(plane_ids == own_dp, jnp.sum(table, axis=0)[None, :], 0), "dp"
    )
    most_rows = jnp.max(plane_counts)
    arrived = jnp.sum(jnp.where(expert_ids == own_expert, table, 0), axis=1)
    earlier = jnp.logical_and(plane_ids < own_dp, expert_ids[:dp_count] == own_expert)
    first_slot = jnp.sum(jnp.where(earlier, plane_counts, 0))
    within = lax.broadcasted_iota(jnp.int32, (expert_count, MOST), 1)
    target = jnp.where(within < arrived[:, None], exclusive(arrived)[:, None] + within, -1).reshape(
        rows_all
    )
    gates_all = lax.all_gather(gate_weights[0], "dp", axis=0, tiled=True)
    gates_all = jnp.concatenate([gates_all, jnp.zeros((rows_all,), gates_all.dtype)])

    def experts(rows, plane_rows):
        slot_ids = lax.broadcasted_iota(jnp.int32, (rows_all, plane_rows), 1)
        place_table = (target[:, None] == slot_ids).astype(jnp.bfloat16)
        plane = lax.dot_general(
            place_table, rows, (((0,), (0,)), ((), ())), preferred_element_type=jnp.float32
        ).astype(jnp.bfloat16)
        slot_rows = lax.all_gather(plane, "dp", axis=0, tiled=True)
        hidden = jnp.maximum(
            jnp.dot(slot_rows, weight_in[0], preferred_element_type=jnp.float32), 0.0
        ).astype(jnp.bfloat16)
        share = jnp.dot(hidden, weight_out[0], preferred_element_type=jnp.float32)
        out = lax.psum_scatter(
            share.astype(jnp.bfloat16), "dp", scatter_dimension=0, tiled=True
        ).astype(jnp.float32)
        gates = lax.dynamic_slice_in_dim(gates_all, first_slot, plane_rows, 0)
        scaled = (gates[:, None] * out).astype(jnp.bfloat16)
        returned = jnp.dot(place_table, scaled, preferred_element_type=jnp.float32)
        return returned.astype(jnp.bfloat16)

    fair = slots_dp + slots_dp // 4
    sent_back = lax.cond(
        most_rows <= fair,
        lambda rows: experts(rows, fair),
        lambda rows: experts(rows, rows_all),
        arrived_rows,
    )
    results = lax.all_to_all(
        sent_back.reshape(expert_count, MOST, width),
        EXPERT,
        split_axis=0,
        concat_axis=0,
        tiled=True,
    ).reshape(rows_all, width)
    combined = lax.dot_general(
        pack_table, results, (((0,), (0,)), ((), ())), preferred_element_type=jnp.float32
    )
    return combined.astype(jnp.bfloat16)


def solution(mesh):
    split = Mesh(
        mesh.devices.reshape(mesh.shape["dp"], 4, 4, 2), ("dp", "expert_0", "expert_1", "expert_2")
    )
    placed = (
        P(DP_EXPERT, None),
        P(None, DP_EXPERT),
        P(),
        P(EXPERT, None, "dp"),
        P(EXPERT, "dp", None),
        P(EXPERT, "dp"),
    )
    return jax.shard_map(
        on_device, mesh=split, in_specs=placed, out_specs=P(DP_EXPERT, None), check_vma=False
    )
```

profile of v0, /device:TPU:1, one launch (start us, length us, event | category | flops | bytes accessed | tf_op | source)
XLA Modules:
  0.0 359.8 jit_solution(15286796204240877624)
XLA Ops:
  6.5 0.0 copy-start
  6.5 0.0 copy-start.1
  6.5 0.9 convert_bitcast_fusion.1
  7.5 0.6 reduce-window.11
  8.1 0.2 slice_reduce_fusion
  8.3 0.1 iota.68
  8.4 0.1 convert_subtract_fusion
  8.5 0.0 copy-done
  8.5 1.5 fusion.21
  10.0 8.6 %all-to-all-start = ((bf16[32,8,2048]{2,1,0:T(8,128)(2,1)}), bf16[32,8,2048]{2,1,0:T(8,128)(2,1)S(1)}, u32[]{:S(2)}, u32[]{:S(2)}) async-start(bf16[32,8,2048]{2,1,0:T(8,128)(2,1)} %fusion.21), calls=%async_computation.2 | async-start | bytes 2097152 | tf_op jit(solution)/shard_map/all_to_all | solution.py:32
  18.6 0.1 broadcast_select_fusion
  18.7 127.2 %psum.14 = s32[32,32]{1,0:T(8,128)S(1)} all-reduce(s32[32,32]{1,0:T(8,128)S(1)} %broadcast_select_fusion), channel_id=1, replica_groups=mesh['dp'=8,'expert_0'=4,'expert_1'=4,'expert_2'=2] {'expert_0','expert_..., use_global_device_ids=true, to_apply=%region_3.4 | all-reduce | flops 1024 | bytes 8192 | tf_op jit(solution)/shard_map/psum | solution.py:37
  145.9 0.1 select_reduce_fusion.2
  146.0 0.1 broadcast_select_fusion.1
  146.1 13.5 %psum.15 = s32[8,32]{1,0:T(8,128)S(1)} all-reduce(s32[8,32]{1,0:T(8,128)S(1)} %broadcast_select_fusion.1), channel_id=1, replica_groups=mesh['dp'=8,'expert_0'=4,'expert_1'=4,'expert_2'=2] {'dp'}, use_global_device_ids=true, to_apply=%region_5.6 | all-reduce | flops 256 | bytes 2048 | tf_op jit(solution)/shard_map/psum | solution.py:39
  159.6 0.7 reduce_max.9
  161.0 0.1 copy.25
  161.1 0.1 reduce-window.18
  161.2 0.0 copy-done.1
  161.2 10.9 %all-gather = f32[1,1024]{1,0:T(1,128)S(1)} all-gather(f32[1,128]{1,0:T(1,128)S(1)} %copy-done.1), channel_id=2, replica_groups=mesh['dp'=8,'expert_0'=4,'expert_1'=4,'expert_2'=2] {'dp'}, dimensions={1}, use_global_device_ids=true | all-gather | bytes 4608 | tf_op jit(solution)/shard_map/all_gather | solution.py:50
  172.0 0.0 all-to-all-done
  172.1 155.2 %conditional.2 = (bf16[256,2048]{1,0:T(8,128)(2,1)S(1)}) conditional(s32[]{:T(128)} %convert_element_type.51, (s32[32]{0:T(128)S(1)}, s32[32,8]{1,0:T(8,128)S(1)}, s32[32,1]{1,0:T(8,128)S(1)}, s32[32,8]{1,0:T(8,128)S(1)}, f32[1024]{0:T(1024)S(1)}, /*index=5*/s32[]{:T(128)}, s32[8]{0:T(128)S(1)}, pred[32]{0:T(512)(128)(4,1)S(1)}, ...), branch_computations={%region_9.12_spmd, %region_12.15_spmd} | conditional | flops 17727356928 | bytes 85999704
  172.1 0.0 all-gather.6.cloned.1.call-start
  172.1 0.1 copy.27
  172.2 0.1 add_select_fusion.1
  172.3 0.1 eq.45
  172.4 1.3 convolution_convert_fusion.3
  173.7 0.0 all-gather.6.cloned.1.call-update
  173.7 0.2 reduce-scatter.5.cloned.1.call-start
  174.0 70.5 %all-gather.6.cloned.1.call-done = bf16[1280,2048]{1,0:T(8,128)(2,1)} async-done(((bf16[160,2048]{1,0:T(8,128)(2,1)}), bf16[1280,2048]{1,0:T(8,128)(2,1)}) %all-gather.6.cloned.1.call-update) | async-done | bytes 5242896 | tf_op jit(solution)/shard_map/cond/branch_1_fun/all_gather | solution.py:59
  244.4 16.9 %convolution_convert_fusion.2 = bf16[1280,2048]{1,0:T(8,128)(2,1)} fusion(bf16[1,1024,2048]{2,1,0:T(8,128)(2,1)} %get-tuple-element.129, bf16[1280,2048]{1,0:T(8,128)(2,1)} %all-gather.6.cloned.1.call-done, bf16[1,2048,1024]{2,1,0:T(8,128)(2,1)} %get-tuple-element.128), kind=kOutput, calls=%fused_computation.19 | convolution fusion | flops 10742661120 | bytes 18874368 | tf_op jit(solution)/shard_map/cond/branch_1_fun/dot_general | solution.py:63
  261.3 0.0 reduce-scatter.5.cloned.1.call-update
  261.4 0.7 select_reduce_fusion.1
  264.0 0.1 pad_dynamic-slice_fusion.1
  264.1 61.4 %reduce-scatter.5.cloned.1.call-done = bf16[160,2048]{1,0:T(8,128)(2,1)} async-done(((bf16[1280,2048]{1,0:T(8,128)(2,1)}), bf16[160,2048]{1,0:T(8,128)(2,1)}) %reduce-scatter.5.cloned.1.call-update) | async-done | bytes 655376 | tf_op jit(solution)/shard_map/cond/branch_1_fun/reduce_scatter | solution.py:64
  325.4 1.6 fusion.15
  327.3 24.3 %all_to_all.10 = bf16[32,8,2048]{2,1,0:T(8,128)(2,1)S(1)} all-to-all(bf16[32,8,2048]{2,1,0:T(8,128)(2,1)S(1)} %bitcast.60), channel_id=1, replica_groups=mesh['dp'=8,'expert_0'=4,'expert_1'=4,'expert_2'=2] {'expert_0','expert_..., dimensions={0} | all-to-all | bytes 2097152 | tf_op jit(solution)/shard_map/all_to_all | solution.py:79
  351.5 1.5 fusion.20
  (11 shorter events, 0.1 us)
Async XLA Ops:
  6.5 2.0 copy-start
  6.5 154.6 %copy-start.1 = (f32[1,128]{1,0:T(1,128)S(1)}, f32[1,128]{1,0:T(1,128)}, u32[]{:S(2)}) copy-start(f32[1,128]{1,0:T(1,128)} %param.13) | copy-start | bytes 1540
  10.0 162.1 %all-to-all-start = ((bf16[32,8,2048]{2,1,0:T(8,128)(2,1)}), bf16[32,8,2048]{2,1,0:T(8,128)(2,1)S(1)}, u32[]{:S(2)}, u32[]{:S(2)}) async-start(bf16[32,8,2048]{2,1,0:T(8,128)(2,1)} %fusion.21), calls=%async_computation.2 | async-start | bytes 2097152 | tf_op jit(solution)/shard_map/all_to_all | solution.py:32
  172.1 72.3 %all-gather.6.cloned.1.call-start = ((), (), s32[]{:S(2)}) async-start(), calls=%async_computation.6 | async-start | bytes 5898240 | tf_op jit(solution)/shard_map/cond/branch_1_fun/all_gather | solution.py:59
  173.7 151.7 %reduce-scatter.5.cloned.1.call-start = ((), (), s32[]{:S(2)}) async-start(), calls=%async_computation.7 | async-start | bytes 5898240 | tf_op jit(solution)/shard_map/cond/branch_1_fun/reduce_scatter | solution.py:64
Sparse Core Ops, SparseCore 0:
  174.7 69.7 all-gather.5
  261.5 63.9 reduce-scatter.4
where the time goes:
time: 360 us
  blocking collectives  176 us (49%)
  waiting for transfers between devices  132 us (37%)
  matrix products  22.7 us (6%)
  between operations  14.1 us (4%)
  starting transfers between devices  8.84 us (2%)
    psum x1, blocking collectives, on_device(): lax.psum(jnp.where(device_ids == own_expert, counts[None, :], 0), EXPERT)  127 us
    all_gather x1, waiting for transfers between devices, experts(): slot_rows = lax.all_gather(plane, 'dp', axis=0, tiled=True)  70.5 us
    reduce_scatter x1, waiting for transfers between devices, experts(): lax.psum_scatter(share.astype(jnp.bfloat16), 'dp', scatter_dimension=0, t...  61.4 us
    all_to_all x1, blocking collectives, on_device(): lax.all_to_all(sent_back.reshape(expert_count, MOST, width), EXPERT, spli...  24.3 us
    dot_general x1, matrix products, experts(): share = jnp.dot(hidden, weight_out[0], preferred_element_type=jnp.float32)  16.9 us
    psum x1, blocking collectives, on_device(): lax.psum(jnp.where(plane_ids == own_dp, jnp.sum(table, axis=0)[None, :],...  13.5 us
    all_gather x1, blocking collectives, on_device(): gates_all = lax.all_gather(gate_weights[0], 'dp', axis=0, tiled=True)  10.9 us
    all_to_all x1, starting transfers between devices, on_device(): lax.all_to_all(packed.reshape(expert_count, MOST, width), EXPERT, split_a...  8.58 us
  transfers between devices with their start and end apart: 3, of which 2 were waited for; matrix products, arithmetic and copies ran while one was open for 1% of the time, Pallas kernels for 0%

commit v1 on v0

--- a/solution.py
+++ b/solution.py
@@ -34,7 +34,10 @@
     ).reshape(rows_all, width)
     device_ids = lax.broadcasted_iota(jnp.int32, (expert_count, expert_count), 0)
     expert_ids = lax.broadcasted_iota(jnp.int32, (expert_count, expert_count), 1)
-    table = lax.psum(jnp.where(device_ids == own_expert, counts[None, :], 0), EXPERT)
+    table = lax.psum(
+        lax.psum(jnp.where(device_ids == own_expert, counts[None, :], 0), "expert_0"),
+        ("expert_1", "expert_2"),
+    )
     plane_ids = lax.broadcasted_iota(jnp.int32, (dp_count, expert_count), 0)
     plane_counts = lax.psum(
         jnp.where(plane_ids == own_dp, jnp.sum(table, axis=0)[None, :], 0), "dp"

time: 360 us -> 276 us (0.77)
  blocking collectives: 176 us -> 92.4 us
    psum x1 -> x2, blocking collectives: 127 us -> 44.4 us  [the longest x1 23.6 us: on_device(): lax.psum(lax.psum(jnp.where(device_ids == own_expert, counts[None, :], 0)...]
where the time goes in v1:
time: 276 us; the launch traced here: 275 us
  waiting for transfers between devices  131 us (47%)
  blocking collectives  92.4 us (33%)
  matrix products  22.7 us (8%)
  between operations  14.1 us (5%)
  starting transfers between devices  8.84 us (3%)
  other arithmetic  3.51 us (1%)
    all_gather x1, waiting for transfers between devices, experts(): slot_rows = lax.all_gather(plane, 'dp', axis=0, tiled=True)  69.3 us
    reduce_scatter x1, waiting for transfers between devices, experts(): lax.psum_scatter(share.astype(jnp.bfloat16), 'dp', scatter_dimension=0, t...  61.3 us
    all_to_all x1, blocking collectives, on_device(): lax.all_to_all(sent_back.reshape(expert_count, MOST, width), EXPERT, spli...  24.3 us
    psum x1, blocking collectives, on_device(): lax.psum(lax.psum(jnp.where(device_ids == own_expert, counts[None, :], 0)...  23.6 us
    psum x1, blocking collectives, on_device(): lax.psum(jnp.where(device_ids == own_expert, counts[None, :], 0), 'expert...  20.8 us
    dot_general x1, matrix products, experts(): share = jnp.dot(hidden, weight_out[0], preferred_element_type=jnp.float32)  16.9 us
    psum x1, blocking collectives, on_device(): lax.psum(jnp.where(plane_ids == own_dp, jnp.sum(table, axis=0)[None, :],...  13.2 us
    all_gather x1, blocking collectives, on_device(): gates_all = lax.all_gather(gate_weights[0], 'dp', axis=0, tiled=True)  10.6 us
  transfers between devices with their start and end apart: 3, of which 2 were waited for; matrix products, arithmetic and copies ran while one was open for 1% of the time, Pallas kernels for 0%

profile of v1, /device:TPU:1, one launch (start us, length us, event | category | flops | bytes accessed | tf_op | source)
XLA Modules:
  0.0 275.2 jit_solution(12779037291223920106)
XLA Ops:
  6.5 0.0 copy-start
  6.5 0.0 copy-start.1
  6.5 0.9 convert_bitcast_fusion.1
  7.5 0.6 reduce-window.11
  8.1 0.2 slice_reduce_fusion
  8.3 0.1 iota.68
  8.4 0.1 convert_subtract_fusion
  8.5 0.0 copy-done
  8.5 1.5 fusion.21
  10.0 8.6 %all-to-all-start = ((bf16[32,8,2048]{2,1,0:T(8,128)(2,1)}), bf16[32,8,2048]{2,1,0:T(8,128)(2,1)S(1)}, u32[]{:S(2)}, u32[]{:S(2)}) async-start(bf16[32,8,2048]{2,1,0:T(8,128)(2,1)} %fusion.21), calls=%async_computation.2 | async-start | bytes 2097152 | tf_op jit(solution)/shard_map/all_to_all | solution.py:32
  18.6 0.1 broadcast_select_fusion
  18.7 20.8 %psum.21 = s32[32,32]{1,0:T(8,128)S(1)} all-reduce(s32[32,32]{1,0:T(8,128)S(1)} %broadcast_select_fusion), channel_id=1, replica_groups=mesh['dp'=8,'expert_0'=4,'expert_1'=4,'expert_2'=2] {'expert_0'}, use_global_device_ids=true, to_apply=%region_3.4 | all-reduce | flops 1024 | bytes 8192 | tf_op jit(solution)/shard_map/psum | solution.py:38
  39.5 23.6 %psum.22 = s32[32,32]{1,0:T(8,128)S(1)} all-reduce(s32[32,32]{1,0:T(8,128)S(1)} %psum.21), channel_id=1, replica_groups=mesh['dp'=8,'expert_0'=4,'expert_1'=4,'expert_2'=2] {'expert_1','expert_2'}, use_global_device_ids=true, to_apply=%region_4.5 | all-reduce | flops 1024 | bytes 8192 | tf_op jit(solution)/shard_map/psum | solution.py:37
  63.1 0.1 select_reduce_fusion.2
  63.2 0.1 broadcast_select_fusion.1
  63.2 13.2 %psum.23 = s32[8,32]{1,0:T(8,128)S(1)} all-reduce(s32[8,32]{1,0:T(8,128)S(1)} %broadcast_select_fusion.1), channel_id=1, replica_groups=mesh['dp'=8,'expert_0'=4,'expert_1'=4,'expert_2'=2] {'dp'}, use_global_device_ids=true, to_apply=%region_6.7 | all-reduce | flops 256 | bytes 2048 | tf_op jit(solution)/shard_map/psum | solution.py:42
  76.5 0.7 reduce_max.9
  77.9 0.1 copy.25
  78.0 0.1 reduce-window.18
  78.0 0.0 copy-done.1
  78.0 10.6 %all-gather = f32[1,1024]{1,0:T(1,128)S(1)} all-gather(f32[1,128]{1,0:T(1,128)S(1)} %copy-done.1), channel_id=2, replica_groups=mesh['dp'=8,'expert_0'=4,'expert_1'=4,'expert_2'=2] {'dp'}, dimensions={1}, use_global_device_ids=true | all-gather | bytes 4608 | tf_op jit(solution)/shard_map/all_gather | solution.py:53
  88.6 0.0 all-to-all-done
  88.6 154.0 %conditional.2 = (bf16[256,2048]{1,0:T(8,128)(2,1)S(1)}) conditional(s32[]{:T(128)} %convert_element_type.51, (s32[32]{0:T(128)S(1)}, s32[32,8]{1,0:T(8,128)S(1)}, s32[32,1]{1,0:T(8,128)S(1)}, s32[32,8]{1,0:T(8,128)S(1)}, f32[1024]{0:T(1024)S(1)}, /*index=5*/s32[]{:T(128)}, s32[8]{0:T(128)S(1)}, pred[32]{0:T(512)(128)(4,1)S(1)}, ...), branch_computations={%region_10.13_spmd, %region_13.16_spmd} | conditional | flops 17727356928 | bytes 85999704
  88.6 0.0 all-gather.6.cloned.1.call-start
  88.7 0.1 copy.27
  88.7 0.1 add_select_fusion.1
  88.8 0.1 eq.45
  88.9 1.3 convolution_convert_fusion.3
  90.2 0.0 all-gather.6.cloned.1.call-update
  90.2 0.2 reduce-scatter.5.cloned.1.call-start
  90.5 69.3 %all-gather.6.cloned.1.call-done = bf16[1280,2048]{1,0:T(8,128)(2,1)} async-done(((bf16[160,2048]{1,0:T(8,128)(2,1)}), bf16[1280,2048]{1,0:T(8,128)(2,1)}) %all-gather.6.cloned.1.call-update) | async-done | bytes 5242896 | tf_op jit(solution)/shard_map/cond/branch_1_fun/all_gather | solution.py:62
  159.8 16.9 %convolution_convert_fusion.2 = bf16[1280,2048]{1,0:T(8,128)(2,1)} fusion(bf16[1,1024,2048]{2,1,0:T(8,128)(2,1)} %get-tuple-element.129, bf16[1280,2048]{1,0:T(8,128)(2,1)} %all-gather.6.cloned.1.call-done, bf16[1,2048,1024]{2,1,0:T(8,128)(2,1)} %get-tuple-element.128), kind=kOutput, calls=%fused_computation.19 | convolution fusion | flops 10742661120 | bytes 18874368 | tf_op jit(solution)/shard_map/cond/branch_1_fun/dot_general | solution.py:66
  176.6 0.0 reduce-scatter.5.cloned.1.call-update
  176.7 0.7 select_reduce_fusion.1
  179.3 0.1 pad_dynamic-slice_fusion.1
  179.4 61.3 %reduce-scatter.5.cloned.1.call-done = bf16[160,2048]{1,0:T(8,128)(2,1)} async-done(((bf16[1280,2048]{1,0:T(8,128)(2,1)}), bf16[160,2048]{1,0:T(8,128)(2,1)}) %reduce-scatter.5.cloned.1.call-update) | async-done | bytes 655376 | tf_op jit(solution)/shard_map/cond/branch_1_fun/reduce_scatter | solution.py:67
  240.8 1.6 fusion.15
  242.6 24.3 %all_to_all.10 = bf16[32,8,2048]{2,1,0:T(8,128)(2,1)S(1)} all-to-all(bf16[32,8,2048]{2,1,0:T(8,128)(2,1)S(1)} %bitcast.60), channel_id=1, replica_groups=mesh['dp'=8,'expert_0'=4,'expert_1'=4,'expert_2'=2] {'expert_0','expert_..., dimensions={0} | all-to-all | bytes 2097152 | tf_op jit(solution)/shard_map/all_to_all | solution.py:82
  266.9 1.5 fusion.20
  (11 shorter events, 0.1 us)
Async XLA Ops:
  6.5 2.0 copy-start
  6.5 71.5 %copy-start.1 = (f32[1,128]{1,0:T(1,128)S(1)}, f32[1,128]{1,0:T(1,128)}, u32[]{:S(2)}) copy-start(f32[1,128]{1,0:T(1,128)} %param.13) | copy-start | bytes 1540
  10.0 78.6 %all-to-all-start = ((bf16[32,8,2048]{2,1,0:T(8,128)(2,1)}), bf16[32,8,2048]{2,1,0:T(8,128)(2,1)S(1)}, u32[]{:S(2)}, u32[]{:S(2)}) async-start(bf16[32,8,2048]{2,1,0:T(8,128)(2,1)} %fusion.21), calls=%async_computation.2 | async-start | bytes 2097152 | tf_op jit(solution)/shard_map/all_to_all | solution.py:32
  88.6 71.1 %all-gather.6.cloned.1.call-start = ((), (), s32[]{:S(2)}) async-start(), calls=%async_computation.6 | async-start | bytes 5898240 | tf_op jit(solution)/shard_map/cond/branch_1_fun/all_gather | solution.py:62
  90.2 150.5 %reduce-scatter.5.cloned.1.call-start = ((), (), s32[]{:S(2)}) async-start(), calls=%async_computation.7 | async-start | bytes 5898240 | tf_op jit(solution)/shard_map/cond/branch_1_fun/reduce_scatter | solution.py:67
Sparse Core Ops, SparseCore 0:
  91.2 68.4 all-gather.5
  176.8 63.9 reduce-scatter.4
